TPU v7x, 256 devices: a whole 4x4x8 slice. The times are simulated.
256 devices in a mesh: gx: 8 (over z), gy: 32 (over y, x, core).
Axes of the slice: x: 4, y: 4, z: 8, core: 2. Of those that a mesh axis runs over, the one named last changes fastest.
Arguments:
- rhs: float32 [8, 32, 1, 3, 200, 128], P('gx', 'gy'), may hold values from -25 to 25
- stiff_inverse: bfloat16 [8, 32, 1, 1200, 1200], P('gx', 'gy'), may hold values from -2 to 6, as said below
- schur: bfloat16 [8, 32, 1, 1200, 1200], P('gx', 'gy'), may hold values from -2 to 6, as said below
- phi: bfloat16 [8, 32, 1, 24, 1200], P('gx', 'gy'), may hold values from -0.1875 to 0.1875
- coarse_inverse: float32 [1536, 1536], P(('gx', 'gy')), may hold values from -2 to 6, as said below
- incidence: int32 [8, 32, 1, 8], P('gx', 'gy'), may hold values from 0 to 511, as said below
- pairing: int32 [8, 32, 1, 3, 200], P('gx', 'gy'), may hold values from 0 to 199, as said below
Outputs:
- multipliers: float32 [8, 32, 1, 3, 200, 128], P('gx', 'gy')
- reduction: float32 [128], replicated
Inputs may be any that keep to these rules, and one draw needn't show every extreme that they name: `stiff_inverse`: each block is symmetric positive definite. `schur`: each block is symmetric positive definite. `coarse_inverse`: symmetric positive definite. `incidence`: the corners of the subdomain grid, periodic in the first two dimensions, under an arbitrary numbering of the 512 nodes: corner c of subdomain (x, y, z) is the grid point (x + c % 2, y + (c // 2) % 2, z + c // 4), and subdomains that share a grid point name the same node. `pairing`: each row over the last dimension is a permutation of 0 to 199.
All inputs are finite; a program needn't handle non-finite values.
Results may differ from a plain program's by a relative error of at most 0.0027.
Values sent between devices are 32-bit elements; how exact they have to be, the bound alone decides.
A program may use at most 64 MiB of HBM per device.

v0:
```python
import jax
import jax.numpy as jnp
import numpy as np
from jax import lax
from jax.experimental import pallas as pl
from jax.experimental.pallas import tpu as pltpu
from jax.sharding import PartitionSpec as P

F32, BF16 = jnp.float32, jnp.bfloat16
MESH = pl.DeviceIdType.MESH
HIGHEST = lax.Precision.HIGHEST
FACE, ORDER, LOADS = 200, 1200, 128
SHARED = 4 * FACE
ACTIVE_Z = 0.0
NT = (((1,), (1,)), ((), ()))


def assembly_table():
    table = np.zeros((16, 128, 256), np.float32)
    steps = ((0, 0), (1, 0), (-1, 0), (0, 1), (0, -1))
    for p in range(16):
        x, core = p // 2, p % 2
        for block, (ox, oy) in enumerate(steps):
            for c in range(8):
                gx = (x + ox + c % 2) % 8
                y = core + oy + (c // 2) % 2
                z = c // 4
                for i in range(3):
                    if y == -1:
                        m = 128 * z + 96 + gx * 3 + i
                    else:
                        m = 128 * (y // 2) + (y % 2) * 48 + z * 24 + gx * 3 + i
                    table[p, block * 24 + 3 * c + i, m] = 1.0
        for e in range(8):
            table[p, 120 + e, 120 + e] = 1.0
    return table.reshape(2048, 256)


def loop(low, high, step):
    def body(k, carry):
        step(k)
        return carry

    lax.fori_loop(low, high, body, 0)


def halves(x):
    high = x.astype(BF16)
    return high, (x - high.astype(F32)).astype(BF16)


def stacked(x):
    high = x.astype(BF16).astype(F32)
    return jnp.concatenate([high, x - high], axis=0).astype(BF16)


def iota(shape, dim):
    return lax.broadcasted_iota(jnp.int32, shape, dim)


def dot(a, b):
    return jnp.dot(a, b, preferred_element_type=F32)


def kernel(
    rhs, stiff, schur, phi, coarse, inc, pair, table,
    out, red,
    rv, sm, km, ss, ks, ph, phf, phn, phb, pho, cin, call, pin, pf, pn, at,
    yb, tb, tsb, ts, rx0, rx1, rx2, rx3, rx4, snd,
    y0, t0, w0, d0, yq, tq, wm, dm, ds0, dsm,
    px, phx, phxs, clt, ra, mb, rb, sb, rc, pb, rd, cp, c256, ohp, idt, idr, idm, ids, fb0, fb1, fb2, fb3,
    hsem, xs, xr, ps, pr, fs, fr, is1, ir1, is2, ir2, cs, cr, cps, cpr, gs, gr,
):
    gx, gy = lax.axis_index("gx"), lax.axis_index("gy")
    h, core = gy // 2, gy % 2
    p = gx * 2 + core

    def device(x, y):
        return {"gx": x, "gy": y}

    def ring(q):
        return device(q // 2, 2 * h + q % 2)

    def plane(other):
        return device(gx, 2 * other + core)

    xu, xd = device((gx + 1) % 8, gy), device((gx + 7) % 8, gy)
    yu, yd = device(gx, (gy + 1) % 32), device(gx, (gy + 31) % 32)

    def remote(src, dst, send, recv, target):
        return pltpu.make_async_remote_copy(
            src_ref=src, dst_ref=dst, send_sem=send, recv_sem=recv, device_id=target, device_id_type=MESH
        )

    loads = [(rhs, rv), (pair, pin), (phi, ph), (coarse, cin), (schur, sm), (table, at), (stiff, km)]
    fetch = [pltpu.make_async_copy(a, b, hsem.at[i]) for i, (a, b) in enumerate(loads)]
    for f in fetch:
        f.start()

    barrier = pltpu.get_barrier_semaphore()

    def greet(target):
        pl.semaphore_signal(barrier, inc=1, device_id=target, device_id_type=MESH)

    loop(1, 16, lambda k: greet(ring((p + k) % 16)))
    loop(1, 16, lambda k: greet(plane((h + k) % 16)))
    greet(yu)
    greet(yd)

    fetch[0].wait()
    fetch[1].wait()
    pf[...] = jnp.full((8, 256), -1.0, F32)
    pf[0:3, 0:FACE] = pin[...].astype(F32)
    down = iota((FACE, FACE), 0).astype(F32)
    for a in range(2):
        onto = (pf[a : a + 1, 0:FACE] == down).astype(F32)
        snd[400 * a : 400 * a + FACE, :] = jnp.dot(onto, rv[a], precision=HIGHEST, preferred_element_type=F32)

    lane = iota((8, 128), 1)
    mine = jnp.zeros((8, 128), F32)
    for z in range(2):
        base = core * 48 + z * 24 + gx * 3
        node = jnp.full((8, 128), inc[4 * z], jnp.int32)
        mine = jnp.where((lane >= base) & (lane < base + 3), (3 * node + (lane - base)).astype(F32), mine)
    idt[...] = mine
    idr[p] = mine

    fetch[2].wait()
    phf[...] = ph[...].astype(F32)
    fetch[3].wait()
    call[p, 0:6, :] = cin[...]
    call[p, 6:8, :] = jnp.zeros((2, 1536), F32)

    pl.semaphore_wait(barrier, 32)

    def face_copy(src, dst, turn, face):
        rows = pl.ds(FACE * face, FACE)
        target = (xu, xd, yu, yd)[face]
        return remote(src.at[rows], dst.at[rows], xs.at[turn, face], xr.at[turn, face], target)

    first = [face_copy(snd, rx0, 0, f) for f in (0, 2)]
    for c in first:
        c.start()
    pairs = [remote(pf, pn.at[a], ps.at[a], pr.at[a], (xu, yu)[a]) for a in range(2)]
    for c in pairs:
        c.start()

    def started(me, where, src, dst, send, recv):
        def go(k):
            q = (me + k) % 16
            remote(src(q), dst.at[me], send.at[q], recv.at[me], where(q)).start()

        loop(1, 16, go)

    def ended(me, where, src, dst, send, recv):
        def go(k):
            q = (me + k) % 16
            remote(src(q), dst.at[q], send.at[q], recv.at[q], where(q)).wait_recv()

        def sent(k):
            q = (me + k) % 16
            remote(src(q), dst.at[q], send.at[q], recv.at[q], where(q)).wait_send()

        loop(1, 16, go)
        loop(1, 16, sent)

    id1 = (p, ring, lambda q: idt, idr, is1, ir1)
    started(*id1)

    windows = ((0, 256), (128, 512), (384, 640), (512, 896))
    coupling = []
    for block, target in enumerate((xd, xu, yd, yu)):
        low, high = windows[block]
        coupling.append(
            remote(phf.at[:, low:high], phn.at[block, :, low:high], fs.at[block], fr.at[block], target)
        )
    for c in coupling:
        c.start()

    def row_copy(k):
        x = (gx + k) % 8
        return remote(call.at[p], call.at[p], cs.at[k], cr.at[gx], device(x, gy))

    other = device(gx, 2 * h + 1 - core)
    loop(1, 8, lambda k: row_copy(k).start())
    remote(call.at[p], call.at[p], cps.at[gx], cpr.at[gx], other).start()

    for c in pairs:
        c.wait()
    spare = jnp.full((8, 256), -1.0, F32)
    for a, (up, low) in enumerate(((FACE, 0), (312, 112))):
        wide = jnp.concatenate([pf[...] + 1.0, spare + 1.0], axis=1)
        own = pltpu.roll(wide, up, 1)[a : a + 1, :] - 1.0
        top = (own == iota((FACE, 512), 0).astype(F32)).astype(F32)
        col = jnp.transpose(jnp.concatenate([pn[a]] * 16, axis=0))[0:FACE, a : a + 1]
        bottom = (col + float(low) == iota((FACE, 512), 1).astype(F32)).astype(F32)
        px[a] = jnp.concatenate([top, bottom], axis=0).astype(BF16)

    def sent_rows(matrix, result):
        result[0:400, :] = dot(px[0], matrix[0:512, :]).astype(BF16)
        result[400:800, :] = dot(px[1], matrix[288:800, :]).astype(BF16)

    fetch[4].wait()
    sent_rows(sm, ss)

    for c in coupling:
        c.wait()
    at_lane = iota((24, 896), 1)
    for block in range(4):
        keep = (at_lane >= FACE * block) & (at_lane < FACE * (block + 1))
        phf2 = jnp.where(keep, -phn[block], 0.0)
        phn[block] = phf2
    phb[...] = phn[...].reshape(96, 896).astype(BF16)
    full = iota((24, ORDER), 1)
    zone = jnp.where(full < SHARED, 1.0, jnp.where(full < SHARED + FACE, 0.0, ACTIVE_Z))
    pho[...] = (phf[...] * zone).astype(BF16)
    tsb[800:896, :] = jnp.zeros((96, 256), BF16)

    def put(x, dst, rows):
        high, low = halves(x)
        dst[0:rows, 0:128] = high
        dst[0:rows, 128:256] = low

    def product(matrix, chunks, result):
        def chunk(i):
            rows = pl.ds(pl.multiple_of(i * 400, 400), 400)
            both = dot(matrix[rows, :], yb[...])
            result[rows, :] = both[:, 0:128] + both[:, 128:256]

        loop(0, chunks, chunk)

    def field(u, arrived, scale):
        return jnp.concatenate(
            [
                scale * (u[0:SHARED, :] - arrived[...]),
                jnp.zeros((FACE, LOADS), F32),
                (scale * ACTIVE_Z) * u[SHARED + FACE : ORDER, :],
            ],
            axis=0,
        )

    def total(a, b):
        return jnp.sum(a * b, axis=0, keepdims=True)

    def extras(*rows):
        sub = iota((8, 128), 0)
        tile = jnp.zeros((8, 128), F32)
        for i, row in enumerate(rows):
            tile = jnp.where(sub == i, row, tile)
        return tile

    def faces(src, dst, turn):
        return [face_copy(src, dst, turn, f) for f in range(4)]

    def corner_loads(t, tile):
        put(t[...], tb, ORDER)
        put(ts[...], tsb, SHARED)
        own = dot(pho[...], tb[...])
        nearby = dot(phb[...], tsb[...])
        own = 0.5 * (own[:, 0:128] + own[:, 128:256])
        nearby = 0.5 * (nearby[:, 0:128] + nearby[:, 128:256])
        clt[...] = jnp.transpose(jnp.concatenate([own, nearby, tile], axis=0))

    lane256 = iota((8, 256), 1)
    tail = (lane256 % 128) >= 120

    def coarse(turn, after_send, during_b, during_c):
        g = 4 * turn
        a = (p, ring, lambda q: clt.at[pl.ds(pl.multiple_of(8 * q, 8), 8)], ra.at[turn], gs.at[g], gr.at[g])
        started(*a)
        ra[turn, p] = clt[pl.ds(pl.multiple_of(8 * p, 8), 8), :]
        after_send()
        ended(*a)
        got = jnp.concatenate([ra[turn, i] for i in range(16)], axis=1)
        both = dot(stacked(got), at[...])
        mb[...] = both[0:8] + both[8:16]
        b = (h, plane, lambda q: mb, rb.at[turn], gs.at[g + 1], gr.at[g + 1])
        started(*b)
        rb[turn, h] = mb[...]
        during_b()
        ended(*b)
        pieces, sums = [], jnp.zeros((8, 128), F32)
        for i in range(16):
            here, before, after = rb[turn, i], rb[turn, (i + 15) % 16], rb[turn, (i + 1) % 16]
            sums = sums + here[:, 0:128]
            part = jnp.where(lane < 96, here[:, 0:128] + before[:, 128:256], 0.0)
            part = part + jnp.where((lane >= 48) & (lane < 72), pltpu.roll(after[:, 0:128], 80, 1), 0.0)
            part = part + jnp.where((lane >= 72) & (lane < 96), pltpu.roll(after[:, 128:256], 104, 1), 0.0)
            pieces.append(part)
        four = lax.dot_general(
            stacked(jnp.concatenate(pieces, axis=1)), cp[...], NT, preferred_element_type=F32
        )
        sb[...] = (four[0:8, 0:128] + four[0:8, 128:256]) + (four[8:16, 0:128] + four[8:16, 128:256])
        c = (h, plane, lambda q: sb, rc.at[turn], gs.at[g + 2], gr.at[g + 2])
        started(*c)
        rc[turn, h] = sb[...]
        during_c()
        ended(*c)
        got = jnp.concatenate([rc[turn, i] for i in range(16)], axis=1)
        both = dot(stacked(got), ohp[...])
        picked = jnp.where(tail, jnp.concatenate([sums, sums], axis=1), both[0:8] + both[8:16])
        pb[0] = picked[:, 0:128]
        pb[1] = picked[:, 128:256]
        d = (p, ring, lambda q: pb.at[q % 2], rd.at[turn], gs.at[g + 3], gr.at[g + 3])
        started(*d)
        rd[turn, p] = pb[core]
        ended(*d)
        return jnp.transpose(rd[turn].reshape(128, 128))

    def spread(solved):
        high, low = halves(solved)
        both = jnp.concatenate([high, low], axis=1)
        near, far = dot(phx[...], both), dot(phxs[...], both)
        return near[:, 0:128] + near[:, 128:256], far[:, 0:128] + far[:, 128:256]

    for c in first:
        c.wait()
    zeros = jnp.zeros((FACE, LOADS), F32)
    y0[...] = 0.5 * jnp.concatenate(
        [-rx0[0:FACE, :], rv[0], -rx0[2 * FACE : 3 * FACE, :], rv[1], zeros, ACTIVE_Z * rv[2]], axis=0
    )
    put(y0[...], yb, ORDER)
    product(ss, 2, ts)
    product(sm, 3, t0)
    start_energy = total(y0[...], t0[...])
    fetch[5].wait()
    corner_loads(t0, extras(start_energy))

    turn1 = faces(ts, rx1, 1)

    def setup_early():
        for c in turn1:
            c.start()
        ended(*id1)
        idm[...] = sum([idr[i] for i in range(1, 16)], idr[0])
        started(h, plane, lambda q: idm, ids, is2, ir2)
        ids[h] = idm[...]

        def forward(k):
            x = (gx + k) % 8
            slot = 2 * x + core
            remote(call.at[slot], call.at[slot], cs.at[k], cr.at[x], other).wait_recv()
            remote(call.at[slot], call.at[slot], cps.at[x], cpr.at[x], other).start()

        loop(1, 8, forward)

        e = iota((128, 24), 1)
        c = (e * 11) >> 5
        i = e - 3 * c
        to = ((c >> 1) & 1) * 48 + (c >> 2) * 24 + ((gx + (c & 1)) % 8) * 3 + i
        place = (to == iota((128, 24), 0)).astype(BF16)
        phx[...] = jnp.transpose(dot(place, ph[...])).astype(BF16)
        phxs[0:400, :] = dot(px[0], phx[0:512, :]).astype(BF16)
        phxs[400:800, :] = dot(px[1], phx[288:800, :]).astype(BF16)
        fetch[6].wait()
        sent_rows(km, ks)

    def setup_late():
        loop(1, 8, lambda k: row_copy(k).wait_send())

        def swapped(x):
            slot = 2 * x + 1 - core
            copy = remote(call.at[slot], call.at[slot], cps.at[x], cpr.at[x], other)
            copy.wait_recv()
            copy.wait_send()

        loop(0, 8, swapped)
        high, low = halves(call[...].reshape(128, 1536))
        c256[0:128, :] = high
        c256[128:256, :] = low
        ended(h, plane, lambda q: idm, ids, is2, ir2)
        row = iota((1536, 256), 0)
        lanes = iota((1, 128), 1)

        def columns(j):
            pair_ids = [jnp.where(lanes < 96, ids[2 * j + s][0:1, :], -1.0) for s in range(2)]
            wanted = jnp.concatenate(pair_ids, axis=1).astype(jnp.int32)
            pick = (row == wanted).astype(F32).astype(BF16)
            cp[:, pl.ds(pl.multiple_of(j * 256, 256), 256)] = dot(c256[...], pick).astype(BF16)

        loop(0, 8, columns)
        here, after = ids[h][0:1, :], ids[(h + 1) % 16][0:1, :]
        here8, after8 = ids[h], ids[(h + 1) % 16]
        shifted = jnp.where(lane < 48, pltpu.roll(here8, 80, 1), pltpu.roll(after8, 48, 1))[0:1, :]
        wanted = jnp.concatenate([jnp.where(lanes < 96, v, -1.0) for v in (here, shifted)], axis=1)
        wanted = wanted.astype(jnp.int32)

        def picks(j):
            r = iota((128, 256), 0)
            own = 192 * (r >> 4) + 12 * j + 6 * ((r >> 3) & 1) + (r & 7)
            own = jnp.where((r & 7) < 6, own, -2)
            ohp[pl.ds(pl.multiple_of(j * 128, 128), 128), :] = (own == wanted).astype(F32).astype(BF16)

        loop(0, 16, picks)

    def first_direction():
        for c in turn1:
            c.wait()
        w0[...] = field(t0, rx1, 0.5)
        put(w0[...], yb, ORDER)
        product(ks, 2, ds0)
        product(km, 3, d0)

    solved = coarse(0, setup_early, setup_late, first_direction)
    start_energy = solved[120:121, :]
    near, far = spread(solved)
    ds0[...] = ds0[...] + far
    turn2 = faces(ds0, rx2, 2)
    for c in turn2:
        c.start()
    d0[...] = d0[...] + near
    curvature = total(w0[...], d0[...])

    for c in turn2:
        c.wait()
    yq[...] = field(d0, rx2, 0.5)
    put(yq[...], yb, ORDER)
    product(ss, 2, ts)
    product(sm, 3, tq)
    corner_loads(tq, extras(curvature, total(y0[...], tq[...]), total(yq[...], tq[...])))
    turn3 = faces(ts, rx3, 3)

    def send_third():
        for c in turn3:
            c.start()

    def second_direction():
        for c in turn3:
            c.wait()
        wm[...] = field(tq, rx3, 0.5)
        put(wm[...], yb, ORDER)
        product(ks, 2, dsm)
        product(km, 3, dm)

    solved = coarse(1, send_third, lambda: None, second_direction)
    alpha = start_energy / solved[120:121, :]
    energy = start_energy - 2.0 * alpha * solved[121:122, :] + alpha * alpha * solved[122:123, :]
    ratio = 1.0 + energy / start_energy
    near, far = spread(solved)
    snd[...] = ratio * ds0[...] - alpha * (dsm[...] + far)
    turn4 = faces(snd, rx4, 4)
    for c in turn4:
        c.start()
    d0[...] = ratio * d0[...] - alpha * (dm[...] + near)
    curvature = total(ratio * w0[...] - alpha * wm[...], d0[...])
    y0[...] = y0[...] - alpha * yq[...]

    for c in turn4:
        c.wait()
    yq[...] = field(d0, rx4, 0.5)
    put(yq[...], yb, ORDER)
    product(sm, 3, tq)
    fb0[...] = extras(curvature, total(y0[...], tq[...]), total(yq[...], tq[...]))
    last = (p, ring, lambda q: fb0, fb1, gs.at[8], gr.at[8])
    started(*last)
    fb1[p] = fb0[...]
    ended(*last)
    fb2[...] = sum([fb1[i] for i in range(1, 16)], fb1[0])
    last = (h, plane, lambda q: fb2, fb3, gs.at[9], gr.at[9])
    started(*last)
    fb3[h] = fb2[...]
    ended(*last)
    sums = sum([fb3[i] for i in range(1, 16)], fb3[0])
    step = energy / sums[0:1, :]
    final = energy - 2.0 * step * sums[1:2, :] + step * step * sums[2:3, :]
    red[...] = jnp.broadcast_to(final / start_energy, (8, 128))
    for a in range(3):
        rows = slice(FACE * (2 * a + 1), FACE * (2 * a + 2))
        out[a] = (alpha + step * ratio) * w0[rows, :] - (step * alpha) * wm[rows, :]


def local(rhs, stiff, schur, phi, coarse, inc, pair):
    table = jnp.asarray(assembly_table(), BF16)
    v = pltpu.VMEM
    wide, sent = v((ORDER, LOADS), F32), v((SHARED, LOADS), F32)
    dma = pltpu.SemaphoreType.DMA
    scratch = [
        v((3, FACE, LOADS), F32), v((ORDER, ORDER), BF16), v((ORDER, ORDER), BF16),
        v((SHARED, ORDER), BF16), v((SHARED, ORDER), BF16),
        v((24, ORDER), BF16), v((24, ORDER), F32), v((4, 24, 896), F32), v((96, 896), BF16), v((24, ORDER), BF16),
        v((6, 1536), F32), v((16, 8, 1536), F32), v((3, FACE), jnp.int32), v((8, 256), F32), v((2, 8, 256), F32),
        v((2048, 256), BF16),
        v((ORDER, 256), BF16), v((ORDER, 256), BF16), v((896, 256), BF16),
        sent, sent, sent, sent, sent, sent, sent,
        wide, wide, wide, wide, wide, wide, wide, wide, sent, sent,
        v((2, 400, 512), BF16), v((ORDER, 128), BF16), v((SHARED, 128), BF16),
        v((128, 128), F32), v((2, 16, 8, 128), F32), v((8, 256), F32), v((2, 16, 8, 256), F32),
        v((8, 128), F32), v((2, 16, 8, 128), F32), v((2, 8, 128), F32), v((2, 16, 8, 128), F32),
        v((256, 2048), BF16), v((256, 1536), BF16), v((2048, 256), BF16),
        v((8, 128), F32), v((16, 8, 128), F32), v((8, 128), F32), v((16, 8, 128), F32),
        v((8, 128), F32), v((16, 8, 128), F32), v((8, 128), F32), v((16, 8, 128), F32),
        dma((7,)), dma((5, 4)), dma((5, 4)), dma((2,)), dma((2,)), dma((4,)), dma((4,)),
        dma((16,)), dma((16,)), dma((16,)), dma((16,)),
        dma((8,)), dma((8,)), dma((8,)), dma((8,)), dma((10, 16)), dma((10, 16)),
    ]
    any_space = pl.BlockSpec(memory_space=pl.ANY)
    in_vmem = pl.BlockSpec(memory_space=pltpu.VMEM)
    result, reduction = pl.pallas_call(
        kernel,
        out_shape=(jax.ShapeDtypeStruct((3, FACE, LOADS), F32), jax.ShapeDtypeStruct((8, LOADS), F32)),
        in_specs=[any_space] * 5 + [pl.BlockSpec(memory_space=pltpu.SMEM)] + [any_space] * 2,
        out_specs=(in_vmem, in_vmem),
        scratch_shapes=scratch,
        compiler_params=pltpu.CompilerParams(
            collective_id=0, has_side_effects=True, vmem_limit_bytes=60 * 1024 * 1024
        ),
        name="domain_decomposition",
    )(
        rhs[0, 0, 0], stiff[0, 0, 0], schur[0, 0, 0], phi[0, 0, 0], coarse, inc[0, 0, 0], pair[0, 0, 0], table
    )
    return result[None, None, None], reduction[0]


def solution(mesh):
    four = P("gx", "gy", None, None)
    five = P("gx", "gy", None, None, None)
    six = P("gx", "gy", None, None, None, None)
    return jax.shard_map(
        local,
        mesh=mesh,
        in_specs=(six, five, five, five, P(("gx", "gy"), None), four, five),
        out_specs=(six, P()),
        check_vma=False,
    )
```

profile of v0, /device:TPU:1, one launch (start us, length us, event | category | flops | bytes accessed | tf_op | source)
XLA Modules:
  0.0 104.4 jit_solution(1804471569982670845)
XLA Ops:
  0.6 1.3 %copy.12 = s32[1,1,1,3,200]{4,3,2,1,0:T(4,128)} copy(s32[1,1,1,3,200]{4,2,3,1,0:T(1,128)} %param.14) | data formatting | bytes 4800
  1.9 99.6 %domain_decomposition.1 = (f32[3,200,128]{2,1,0:T(8,128)}, f32[8,128]{1,0:T(8,128)}) custom-call(f32[3,200,128]{2,1,0:T(8,128)} %bitcast.13, bf16[1200,1200]{1,0:T(8,128)(2,1)} %bitcast.11, bf16[1200,1200]{1,0:T(8,128)(2,1)} %bitcast.12, bf16[24,1200]{1,0:T(8,128)(2,1)} %bitcast.15, f32[6,1536]{1,0:T(8,128)} %coarse.1, s32[8]{0:T(128)} %bitcast.17, ...), custom_call_target="tpu_custom_call" | custom-call | tf_op jit(solution)/shard_map/domain_decomposition/pallas_call | solution.py:498
  101.5 1.2 %slice_bitcast_fusion = f32[128]{0:T(128)} fusion(f32[8,128]{1,0:T(8,128)} %get-tuple-element.5), kind=kLoop, calls=%fused_computation.1 | loop fusion | bytes 1024 | tf_op jit(solution)/shard_map/squeeze | solution.py:511
  102.7 1.7 %copy.14 = f32[1,1,1,3,200,128]{5,4,3,2,1,0:T(8,128)} copy(f32[1,1,1,3,200,128]{5,4,3,2,1,0:T(8,128)} %bitcast.14) | data formatting | bytes 614400
where the time goes:
time: 105 us; the launch traced here: 104 us
  Pallas kernels  99.6 us (95%)
  local copies, waits for them, and re-layouts  4.17 us (4%)
    pallas_call x1, Pallas kernels, local(): pl.pallas_call(kernel, out_shape=(jax.ShapeDtypeStruct((3, FACE, LOADS),...  99.6 us
    unnamed x2, local copies, waits for them, and re-layouts  2.98 us

commit v1 on v0

v1 whole, which is shorter than its diff:
```python
import jax
import jax.numpy as jnp
import numpy as np
from jax import lax
from jax.experimental import pallas as pl
from jax.experimental.pallas import tpu as pltpu
from jax.sharding import PartitionSpec as P

F32, BF16 = jnp.float32, jnp.bfloat16
MESH = pl.DeviceIdType.MESH
HIGHEST = lax.Precision.HIGHEST
FACE, ORDER, LOADS = 200, 1200, 128
SHARED = 4 * FACE
ACTIVE_Z = 0.0
NT = (((1,), (1,)), ((), ()))


def assembly_table():
    table = np.zeros((16, 128, 256), np.float32)
    steps = ((0, 0), (1, 0), (-1, 0), (0, 1), (0, -1))
    for p in range(16):
        x, core = p // 2, p % 2
        for block, (ox, oy) in enumerate(steps):
            for c in range(8):
                gx = (x + ox + c % 2) % 8
                y = core + oy + (c // 2) % 2
                z = c // 4
                for i in range(3):
                    if y == -1:
                        m = 128 * z + 96 + gx * 3 + i
                    else:
                        m = 128 * (y // 2) + (y % 2) * 48 + z * 24 + gx * 3 + i
                    table[p, block * 24 + 3 * c + i, m] = 1.0
        for e in range(8):
            table[p, 120 + e, 120 + e] = 1.0
    return table.reshape(2048, 256)


def order_table():
    table = np.zeros((384, 768), np.float32)
    for core in range(2):
        for slot in range(11):
            for y in range(4):
                for z in range(2):
                    for i in range(3):
                        chip, half = divmod(core + 1 + y, 2)
                        lane = chip * 128 + half * 48 + z * 24 + (slot - 1) % 8 * 3 + i
                        table[lane, 384 * core + slot * 24 + y * 6 + z * 3 + i] = 1.0
    return table


def loop(low, high, step):
    def body(k, carry):
        step(k)
        return carry

    lax.fori_loop(low, high, body, 0)


def halves(x):
    high = x.astype(BF16)
    return high, (x - high.astype(F32)).astype(BF16)


def stacked(x):
    high = x.astype(BF16).astype(F32)
    return jnp.concatenate([high, x - high], axis=0).astype(BF16)


def iota(shape, dim):
    return lax.broadcasted_iota(jnp.int32, shape, dim)


def dot(a, b):
    return jnp.dot(a, b, preferred_element_type=F32)


def kernel(
    rhs, stiff, schur, phi, coarse, inc, pair, table, order,
    out, red,
    rv, sm, km, ss, ks, ph, phf, phn, cin, packed, call, pin, pf, pn, at, ot,
    yb, tb, ts, rx0, rx1, rx2, rx3, rx4, snd,
    y0, t0, w0, d0, yp, yq, tq, wm, dm, tp,
    px, pef, pe, pet, big, clt, cl0, cl1, clm,
    ra, mb, rb, sb, rc, pb, rd, cp, c256, ohp, idt, idr, idm, ids, fb0, fb1, fb2, fb3,
    hsem, xs, xr, ps, pr, fs, fr, ns, nr, cs, cr, gs, gr,
):
    gx, gy = lax.axis_index("gx"), lax.axis_index("gy")
    h, core = gy // 2, gy % 2
    p = gx * 2 + core

    def device(x, y):
        return {"gx": x, "gy": y}

    def ring(q):
        return device(q >> 1, 2 * h + (q & 1))

    def plane(other):
        return device(gx, 2 * other + core)

    xu, xd = device((gx + 1) & 7, gy), device((gx + 7) & 7, gy)
    yu, yd = device(gx, (gy + 1) & 31), device(gx, (gy + 31) & 31)

    def remote(src, dst, send, recv, target):
        return pltpu.make_async_remote_copy(
            src_ref=src, dst_ref=dst, send_sem=send, recv_sem=recv, device_id=target, device_id_type=MESH
        )

    loads = [(rhs, rv), (pair, pin), (phi, ph), (coarse, cin), (schur, sm), (table, at), (stiff, km), (order, ot)]
    fetch = [pltpu.make_async_copy(a, b, hsem.at[i]) for i, (a, b) in enumerate(loads)]
    for f in fetch:
        f.start()

    barrier = pltpu.get_barrier_semaphore()

    def greet(target):
        pl.semaphore_signal(barrier, inc=1, device_id=target, device_id_type=MESH)

    loop(1, 16, lambda k: greet(ring((p + k) & 15)))
    loop(1, 16, lambda k: greet(plane((h + k) & 15)))
    greet(yu)
    greet(yd)

    fetch[0].wait()
    fetch[1].wait()
    pf[...] = jnp.full((8, 256), -1000.0, F32)
    for a in range(2):
        pf[a : a + 1, 0:FACE] = pin[a].astype(F32)
    down = iota((FACE, FACE), 0).astype(F32)
    for a in range(2):
        onto = (pf[a : a + 1, 0:FACE] == down).astype(F32)
        snd[400 * a : 400 * a + FACE, :] = jnp.dot(onto, rv[a], precision=HIGHEST, preferred_element_type=F32)

    lane = iota((8, 128), 1)
    mine = jnp.zeros((8, 128), F32)
    for z in range(2):
        base = core * 48 + z * 24 + gx * 3
        node = jnp.full((8, 128), inc[4 * z], jnp.int32)
        mine = jnp.where((lane >= base) & (lane < base + 3), (3 * node + (lane - base)).astype(F32), mine)
    idt[...] = mine
    idr[p] = mine

    fetch[2].wait()
    phf[...] = ph[...].astype(F32)
    fetch[3].wait()
    for k in range(12):
        packed[p, 6 * k : 6 * k + 6, :] = cin[:, 128 * k : 128 * k + 128]
    call[...] = jnp.zeros((16, 8, 1536), F32)

    full = iota((24, ORDER), 1)
    zone = jnp.where(full < SHARED, 1.0, jnp.where(full < SHARED + FACE, 0.0, ACTIVE_Z))
    pef[...] = jnp.zeros((120, ORDER), F32)
    pef[0:24, :] = phf[...] * zone
    r, m = iota((128, 128), 0), iota((128, 128), 1)
    block = (r * 683) >> 14
    e = r - 24 * block
    c = (e * 11) >> 5
    over = 1 + jnp.where(block == 1, 1, 0) - jnp.where(block == 2, 1, 0) + (c & 1)
    up = 1 + jnp.where(block == 3, 1, 0) - jnp.where(block == 4, 1, 0) + ((c >> 1) & 1)
    to = over * 24 + up * 6 + (c >> 2) * 3 + (e - 3 * c)
    place = ((to == m) & (r < 120)).astype(F32).astype(BF16)

    pl.semaphore_wait(barrier, 32)

    def face_copy(src, dst, turn, face):
        rows = pl.ds(FACE * face, FACE)
        return remote(src.at[rows], dst.at[rows], xs.at[turn], xr.at[turn], (xu, xd, yu, yd)[face])

    for a in range(2):
        remote(pf, pn.at[a], ps.at[0], pr.at[0], (xu, yu)[a]).start()
    for f in (0, 2):
        face_copy(snd, rx0, 0, f).start()
    windows = ((0, 384), (128, 512), (384, 768), (512, 896))
    for blk, target in enumerate((xd, xu, yd, yu)):
        low, high = windows[blk]
        remote(phf.at[:, low:high], phn.at[blk, :, low:high], fs.at[0], fr.at[0], target).start()

    def far(step, size):
        return min(step, size - step)

    ring_steps = sorted(((dx, dc) for dx in range(8) for dc in (1, 0)), key=lambda d: -far(d[0], 8))
    ring_others = [2 * ((gx + dx) & 7) + ((core + dc) & 1) for dx, dc in ring_steps if dx or dc]
    plane_steps = sorted(
        ((dy, dx) for dy in range(4) for dx in range(4)), key=lambda d: -far(d[0], 4) - far(d[1], 4)
    )
    plane_others = [4 * (((h >> 2) + dy) & 3) + ((h + dx) & 3) for dy, dx in plane_steps if dy or dx]

    def started(me, where, src, dst, send, recv):
        for q in ring_others if where is ring else plane_others:
            remote(src(q), dst.at[me], send, recv, where(q)).start()

    def ended(dst, send, recv):
        all_blocks = remote(dst.at[0:15], dst.at[0:15], send, recv, xu)
        all_blocks.wait_recv()
        all_blocks.wait_send()

    started(p, ring, lambda q: idt, idr, ns.at[0], nr.at[0])

    other = device(gx, 2 * h + 1 - core)

    def rows_to(slot, target, turn):
        return remote(packed.at[slot], packed.at[slot], cs.at[turn], cr.at[turn], target)

    for k in (1, 7, 2, 6):
        rows_to(p, device((gx + k) & 7, gy), 0).start()
    rows_to(p, other, 2).start()

    def rows_in(count, turn):
        some = packed.at[0:count]
        arrived = remote(some, some, cs.at[turn], cr.at[turn], xu)
        arrived.wait_recv()
        arrived.wait_send()

    both_pairs = remote(pn, pn, ps.at[0], pr.at[0], xu)
    both_pairs.wait_recv()
    both_pairs.wait_send()
    for a, (up, low, shift) in enumerate(((FACE, 0, 0), (344, 144, 16))):
        wide = jnp.concatenate([pf[...], jnp.full((8, 384), -1000.0, F32)], axis=1)
        own = pltpu.roll(wide, up, 1)[a : a + 1, :]
        long = jnp.concatenate([pn[a], jnp.full((8, 256), -1000.0, F32)], axis=1)
        col = jnp.transpose(pltpu.roll(long, FACE + shift, 1))[:, a : a + 1]
        row = (iota((512, 640), 0) - shift).astype(F32)
        at_col = (iota((512, 640), 1) - low).astype(F32)
        px[a] = jnp.where((own == row) | (col == at_col), 1.0, 0.0).astype(BF16)

    def sent_x_rows(matrix, result):
        result[0:400, :] = dot(px[0, 0:400, :], matrix[0:640, :]).astype(BF16)

    def sent_y_rows(matrix, result):
        result[400:800, :] = dot(px[1, 16:416, :], matrix[256:896, :]).astype(BF16)

    def put(x, dst):
        high, low = halves(x)
        dst[:, 0:128] = high
        dst[:, 128:256] = low

    def joined(both):
        return both[:, 0:128] + both[:, 128:256]

    def product(matrix, chunks, result):
        def chunk(i):
            rows = pl.ds(pl.multiple_of(i * 400, 400), 400)
            result[rows, :] = joined(dot(matrix[rows, :], yb[...]))

        loop(0, chunks, chunk)

    def field(u, arrived, scale):
        return jnp.concatenate(
            [
                scale * (u[0:SHARED, :] - arrived[...]),
                jnp.zeros((FACE, LOADS), F32),
                (scale * ACTIVE_Z) * u[SHARED + FACE : ORDER, :],
            ],
            axis=0,
        )

    def total(a, b):
        return jnp.sum(a * b, axis=0, keepdims=True)

    def extras(*rows, size=8):
        sub = iota((size, 128), 0)
        tile = jnp.zeros((size, 128), F32)
        for i, row in enumerate(rows):
            tile = jnp.where(sub == i, row, tile)
        return tile

    def send_faces(src, dst, turn):
        for f in range(4):
            face_copy(src, dst, turn, f).start()

    def wait_faces(dst, turn):
        whole = remote(dst, dst, xs.at[turn], xr.at[turn], xu)
        whole.wait_recv()
        whole.wait_send()

    fetch[4].wait()
    sent_x_rows(sm, ss)

    half = remote(rx0.at[0:400], rx0.at[0:400], xs.at[0], xr.at[0], xu)
    half.wait_recv()
    half.wait_send()
    zeros = jnp.zeros((FACE, LOADS), F32)
    y0[...] = 0.5 * jnp.concatenate(
        [-rx0[0:FACE, :], rv[0], -rx0[2 * FACE : 3 * FACE, :], rv[1], zeros, ACTIVE_Z * rv[2]], axis=0
    )
    put(y0[...], yb)
    product(sm, 3, t0)
    start_energy = total(y0[...], t0[...])

    quarters = remote(phn.at[:, :, 0:384], phn.at[:, :, 0:384], fs.at[0], fr.at[0], xu)
    quarters.wait_recv()
    quarters.wait_send()
    at_lane = iota((24, 896), 1)
    blocks = []
    for blk in range(4):
        keep = (at_lane >= FACE * blk) & (at_lane < FACE * (blk + 1))
        blocks.append(jnp.where(keep, -phn[blk], 0.0))
    along_x = jnp.concatenate(blocks[0:2], axis=0)[:, 0:512].astype(BF16)
    along_y = jnp.concatenate(blocks[2:4], axis=0)[:, 384:896].astype(BF16)
    pef[24:72, 0:640] = dot(along_x, px[0])
    pef[72:120, 256:896] = dot(along_y, px[1])
    pe[...] = pef[...].astype(BF16)

    def corner_loads(t, result):
        put(t[...], tb)
        result[...] = 0.5 * joined(dot(pe[...], tb[...]))

    fetch[5].wait()
    corner_loads(t0, cl0)

    def coarse(turn, loads, tile, during_a, during_b, during_c, during_d):
        g = 4 * turn
        clt[...] = jnp.transpose(jnp.concatenate([loads, tile], axis=0))
        started(
            p, ring, lambda q: clt.at[pl.ds(pl.multiple_of(8 * q, 8), 8)], ra.at[turn], gs.at[0], gr.at[g]
        )
        ra[turn, p] = clt[pl.ds(pl.multiple_of(8 * p, 8), 8), :]
        during_a()
        ended(ra.at[turn], gs.at[0], gr.at[g])
        got = jnp.concatenate([ra[turn, i] for i in range(16)], axis=1)
        both = dot(stacked(got), at[...])
        mb[...] = both[0:8] + both[8:16]
        started(h, plane, lambda q: mb, rb.at[turn], gs.at[1], gr.at[g + 1])
        rb[turn, h] = mb[...]
        during_b()
        ended(rb.at[turn], gs.at[1], gr.at[g + 1])
        pieces, sums = [], jnp.zeros((8, 128), F32)
        for i in range(16):
            here, before, after = rb[turn, i], rb[turn, (i + 15) % 16], rb[turn, (i + 1) % 16]
            sums = sums + here[:, 0:128]
            part = jnp.where(lane < 96, here[:, 0:128] + before[:, 128:256], 0.0)
            part = part + jnp.where((lane >= 48) & (lane < 72), pltpu.roll(after[:, 0:128], 80, 1), 0.0)
            part = part + jnp.where((lane >= 72) & (lane < 96), pltpu.roll(after[:, 128:256], 104, 1), 0.0)
            pieces.append(part)
        four = lax.dot_general(
            stacked(jnp.concatenate(pieces, axis=1)), cp[...], NT, preferred_element_type=F32
        )
        sb[...] = joined(four[0:8]) + joined(four[8:16])
        started(h, plane, lambda q: sb, rc.at[turn], gs.at[0], gr.at[g + 2])
        rc[turn, h] = sb[...]
        during_c()
        ended(rc.at[turn], gs.at[0], gr.at[g + 2])
        got = jnp.concatenate([rc[turn, i] for i in range(16)], axis=1)
        both = dot(stacked(got), ohp[...])
        picked = both[0:8] + both[8:16]
        for q in range(16):
            first, by = divmod(24 * (q // 2), 128)
            at_tile = 384 * (q % 2) + 128 * first
            one = picked[:, at_tile : at_tile + 128]
            if by:
                two = picked[:, at_tile + 128 : at_tile + 256]
                one = jnp.where(lane < 128 - by, pltpu.roll(one, 128 - by, 1), pltpu.roll(two, 128 - by, 1))
            pb[q] = jnp.where(lane < 120, one, sums)
        started(p, ring, lambda q: pb.at[q], rd.at[turn], gs.at[1], gr.at[g + 3])
        rd[turn, p] = pb[p]
        during_d()
        ended(rd.at[turn], gs.at[1], gr.at[g + 3])
        solved = jnp.transpose(rd[turn].reshape(128, 128))
        high, low = halves(solved)
        corners = joined(dot(place, jnp.concatenate([high, low], axis=1)))
        return solved[120:128, :], corners

    def a0():
        rows_in(4, 0)
        below, above = 2 * ((gx + 6) & 7) + core, 2 * ((gx + 2) & 7) + core
        rows_to(below, xu, 1).start()
        rows_to(above, xd, 1).start()
        rows_to(below, device((gx + 2) & 7, gy), 1).start()
        sent_y_rows(sm, ss)
        product(ss, 2, ts)
        send_faces(ts, rx1, 1)
        ended(idr, ns.at[0], nr.at[0])
        idm[...] = sum([idr[i] for i in range(1, 16)], idr[0])
        started(h, plane, lambda q: idm, ids, ns.at[1], nr.at[1])
        ids[h] = idm[...]
        rows_in(3, 1)
        for k in range(1, 8):
            rows_to(2 * ((gx + k) & 7) + core, other, 2).start()
        fetch[6].wait()
        sent_x_rows(km, ks)

    def b0():
        rows_in(8, 2)
        for slot in range(16):
            for k in range(12):
                call[slot, 0:6, 128 * k : 128 * k + 128] = packed[slot, 6 * k : 6 * k + 6, :]
        high, low = halves(call[...].reshape(128, 1536))
        c256[0:128, :] = high
        c256[128:256, :] = low
        ended(ids, ns.at[1], nr.at[1])
        row = iota((1536, 256), 0)
        lanes = iota((1, 128), 1)

        def columns(j):
            pair_ids = [jnp.where(lanes < 96, ids[2 * j + s][0:1, :], -1.0) for s in range(2)]
            wanted = jnp.concatenate(pair_ids, axis=1).astype(jnp.int32)
            pick = (row == wanted).astype(F32).astype(BF16)
            cp[:, pl.ds(pl.multiple_of(j * 256, 256), 256)] = dot(c256[...], pick).astype(BF16)

        loop(0, 8, columns)

    def direction(t, arrived, w, turn, result):
        wait_faces(arrived, turn)
        w[...] = field(t, arrived, 0.5)
        put(w[...], yb)
        product(ks, 2, ts)
        send_faces(ts, result, turn + 1)
        return joined(dot(ph[...], yb[...]))

    kept = {}

    def c0():
        sent_y_rows(km, ks)
        kept["w0"] = direction(t0, rx1, w0, 1, rx2)
        nearby = jnp.concatenate([ids[(h + 15) & 15], ids[h], ids[(h + 1) & 15]], axis=1)
        fetch[7].wait()
        found = dot(stacked(nearby), ot[...])
        wanted = (found[0:1] + found[8:9]).astype(jnp.int32)

        def picks(j):
            rr = iota((128, 768), 0)
            own = 192 * (rr >> 4) + 12 * j + 6 * ((rr >> 3) & 1) + (rr & 7)
            own = jnp.where((rr & 7) < 6, own, -2)
            ohp[pl.ds(pl.multiple_of(j * 128, 128), 128), :] = (own == wanted).astype(F32).astype(BF16)

        loop(0, 16, picks)
        pet[...] = jnp.transpose(jnp.concatenate([pef[...], jnp.zeros((8, ORDER), F32)], axis=0)).astype(BF16)

        def chunk(i):
            rows = pl.ds(pl.multiple_of(i * 400, 400), 400)
            tp[rows, :] = dot(sm[rows, :], pet[...])

        loop(0, 3, chunk)

    def operator():
        put(tp[...], tb)
        through = 0.25 * joined(dot(pe[...], tb[...]))
        through = jnp.concatenate([through, jnp.zeros((8, 128), F32)], axis=0)
        high, low = halves(through)
        big[:, 0:128] = high
        big[:, 128:256] = low

    def second(d, arrived, turn, result):
        wait_faces(arrived, turn)
        yp[...] = field(d, arrived, 0.5)
        put(yp[...], yb)
        product(sm, 3, tp)
        corner_loads(tp, result)

    def coupled(corners):
        high, low = halves(corners)
        wide = jnp.concatenate([high, low], axis=1)
        return joined(dot(big[...], jnp.concatenate([wide, wide], axis=0)))[0:120]

    def d_first():
        product(km, 3, d0)
        operator()
        second(d0, rx2, 2, clm)
        kept["c00"] = total(w0[...], d0[...])
        kept["k1"] = total(t0[...], yp[...])
        kept["k2"] = total(yp[...], tp[...])

    sums, g0 = coarse(0, cl0[...], extras(start_energy), a0, b0, c0, d_first)
    start_energy = sums[0:1, :]
    g0x = g0[0:120]
    cl1[...] = clm[...] + coupled(g0)
    c00 = kept["c00"] + total(kept["w0"], g0[0:24])
    k1 = kept["k1"] + total(cl0[...], g0x)
    k2 = kept["k2"] + total(clm[...] + cl1[...], g0x)

    def a1():
        high, low = halves(0.5 * g0)
        yq[...] = yp[...] + joined(dot(pet[...], jnp.concatenate([high, low], axis=1)))
        put(yq[...], yb)
        product(ss, 2, ts)
        send_faces(ts, rx3, 3)
        product(sm, 3, tq)

    def b1():
        kept["wm"] = direction(tq, rx3, wm, 3, rx4)
        product(km, 3, dm)
        kept["c01"] = total(w0[...], dm[...])
        kept["c10"] = total(wm[...], d0[...]) + total(kept["wm"], g0[0:24])
        kept["c11"] = total(wm[...], dm[...])

    def c1():
        second(dm, rx4, 4, clm)
        kept["m1"] = total(t0[...], yp[...])
        kept["m2"] = total(tq[...], yp[...])
        kept["m3"] = total(yp[...], tp[...])

    sums, gm = coarse(1, cl1[...], extras(c00, k1, k2), a1, b1, c1, lambda: None)
    gmx = gm[0:120]
    alpha = start_energy / sums[0:1, :]
    energy = start_energy - 2.0 * alpha * sums[1:2, :] + alpha * alpha * sums[2:3, :]
    ratio = 1.0 + energy / start_energy
    c01 = kept["c01"] + kept["c10"] + total(kept["w0"], gm[0:24])
    c11 = kept["c11"] + total(kept["wm"], gm[0:24])
    m1 = kept["m1"] + total(cl0[...], gmx)
    m2 = kept["m2"] + total(cl1[...], gmx)
    m3 = kept["m3"] + total(2.0 * clm[...] + coupled(gm), gmx)
    curvature = ratio * ratio * c00 - ratio * alpha * c01 + alpha * alpha * c11
    cross = ratio * (k1 - alpha * k2) - alpha * (m1 - alpha * m2)
    square = ratio * ratio * k2 - 2.0 * ratio * alpha * m2 + alpha * alpha * m3
    fb0[...] = extras(curvature, cross, square, size=4)
    started(p, ring, lambda q: fb0, fb1, gs.at[0], gr.at[8])
    fb1[p] = fb0[...]
    ended(fb1, gs.at[0], gr.at[8])
    fb2[...] = sum([fb1[i] for i in range(1, 16)], fb1[0])
    started(h, plane, lambda q: fb2, fb3, gs.at[1], gr.at[9])
    fb3[h] = fb2[...]
    ended(fb3, gs.at[1], gr.at[9])
    sums = sum([fb3[i] for i in range(1, 16)], fb3[0])
    step = energy / sums[0:1, :]
    final = energy - 2.0 * step * sums[1:2, :] + step * step * sums[2:3, :]
    red[...] = final / start_energy
    for a in range(3):
        rows = slice(FACE * (2 * a + 1), FACE * (2 * a + 2))
        out[a] = (alpha + step * ratio) * w0[rows, :] - (step * alpha) * wm[rows, :]


def hand_over(a, b, out, red):
    out[...] = a[...]
    red[...] = b[...]


def local(rhs, stiff, schur, phi, coarse, inc, pair):
    table, order = jnp.asarray(assembly_table(), BF16), jnp.asarray(order_table(), BF16)
    v = pltpu.VMEM
    wide, sent = v((ORDER, LOADS), F32), v((SHARED, LOADS), F32)
    dma = pltpu.SemaphoreType.DMA
    tile, group = v((8, 128), F32), v((16, 8, 128), F32)
    scratch = [
        v((3, FACE, LOADS), F32), v((ORDER, ORDER), BF16), v((ORDER, ORDER), BF16),
        v((SHARED, ORDER), BF16), v((SHARED, ORDER), BF16),
        v((24, ORDER), BF16), v((24, ORDER), F32), v((4, 24, 896), F32),
        v((6, 1536), F32), v((16, 72, 128), F32), v((16, 8, 1536), F32), v((3, 1, FACE), jnp.int32), v((8, 256), F32), v((2, 8, 256), F32),
        v((2048, 256), BF16), v((384, 768), BF16),
        v((ORDER, 256), BF16), v((ORDER, 256), BF16),
        sent, sent, sent, sent, sent, sent, sent,
        wide, wide, wide, wide, wide, wide, wide, wide, wide, wide,
        v((2, 512, 640), BF16), v((120, ORDER), F32), v((120, ORDER), BF16), v((ORDER, 128), BF16),
        v((128, 256), BF16), v((128, 128), F32), v((120, 128), F32), v((120, 128), F32), v((120, 128), F32),
        v((2, 16, 8, 128), F32), v((8, 256), F32), v((2, 16, 8, 256), F32),
        tile, v((2, 16, 8, 128), F32), group, v((2, 16, 8, 128), F32),
        v((256, 2048), BF16), v((256, 1536), BF16), v((2048, 768), BF16),
        tile, group, tile, group,
        v((4, 128), F32), v((16, 4, 128), F32), v((4, 128), F32), v((16, 4, 128), F32),
        dma((8,)), dma((5,)), dma((5,)), dma((1,)), dma((1,)), dma((1,)), dma((1,)),
        dma((2,)), dma((2,)), dma((3,)), dma((3,)), dma((2,)), dma((10,)),
    ]
    any_space = pl.BlockSpec(memory_space=pl.ANY)
    in_vmem = pl.BlockSpec(memory_space=pltpu.VMEM)
    shapes = (jax.ShapeDtypeStruct((3, FACE, LOADS), F32), jax.ShapeDtypeStruct((1, LOADS), F32))
    result, reduction = pl.pallas_call(
        kernel,
        out_shape=shapes,
        in_specs=[any_space] * 5 + [pl.BlockSpec(memory_space=pltpu.SMEM)] + [any_space] * 3,
        out_specs=(in_vmem, in_vmem),
        scratch_shapes=scratch,
        compiler_params=pltpu.CompilerParams(
            collective_id=0, has_side_effects=True, vmem_limit_bytes=60 * 1024 * 1024
        ),
        name="domain_decomposition",
    )(
        rhs[0, 0, 0], stiff[0, 0, 0], schur[0, 0, 0], phi[0, 0, 0], coarse, inc[0, 0, 0],
        pair.reshape(3, 1, FACE), table, order,
    )
    result, reduction = pl.pallas_call(
        hand_over, out_shape=shapes, in_specs=[in_vmem] * 2, out_specs=(in_vmem, in_vmem), name="hand_over"
    )(result, reduction)
    return result[None, None, None], reduction[0]


def solution(mesh):
    four = P("gx", "gy", None, None)
    five = P("gx", "gy", None, None, None)
    six = P("gx", "gy", None, None, None, None)
    return jax.shard_map(
        local,
        mesh=mesh,
        in_specs=(six, five, five, five, P(("gx", "gy"), None), four, five),
        out_specs=(six, P()),
        check_vma=False,
    )
```

time: 105 us -> 76.9 us (0.73)
  Pallas kernels: 99.6 us -> 76.2 us
  local copies, waits for them, and re-layouts: 4.17 us -> 0 us
    pallas_call x1 -> x2, Pallas kernels: 99.6 us -> 76.2 us  [the longest x1 74.5 us: local(): pl.pallas_call(kernel, out_shape=shapes, in_specs=[any_space] * 5 + [pl.B...]
    unnamed x2 -> x0, local copies, waits for them, and re-layouts: 2.98 us -> none
    squeeze x1 -> x0, local copies, waits for them, and re-layouts: 1.19 us -> none  [local(): return (result[None, None, None], reduction[0])]
where the time goes in v1:
time: 76.9 us; the launch traced here: 76.8 us
  Pallas kernels  76.2 us (99%)
    pallas_call x1, Pallas kernels, local(): pl.pallas_call(kernel, out_shape=shapes, in_specs=[any_space] * 5 + [pl.B...  74.5 us
    pallas_call x1, Pallas kernels, local(): pl.pallas_call(hand_over, out_shape=shapes, in_specs=[in_vmem] * 2, out_s...  1.71 us

profile of v1, /device:TPU:1, one launch (start us, length us, event | category | flops | bytes accessed | tf_op | source)
XLA Modules:
  0.0 76.8 jit_solution(9136629456108230880)
XLA Ops:
  0.6 74.5 %domain_decomposition.1 = (f32[3,200,128]{2,1,0:T(8,128)}, f32[1,128]{1,0:T(1,128)}) custom-call(f32[3,200,128]{2,1,0:T(8,128)} %bitcast.10, bf16[1200,1200]{1,0:T(8,128)(2,1)} %bitcast.8, bf16[1200,1200]{1,0:T(8,128)(2,1)} %bitcast.9, bf16[24,1200]{1,0:T(8,128)(2,1)} %bitcast.11, f32[6,1536]{1,0:T(8,128)} %coarse.1, s32[8]{0:T(128)} %bitcast.13, ...), custom_call_target="tpu_custom_call" | custom-call | tf_op jit(solution)/shard_map/domain_decomposition/pallas_call | solution.py:555
  75.1 1.7 %hand_over.1 = (f32[3,200,128]{2,1,0:T(8,128)}, f32[1,128]{1,0:T(1,128)}) custom-call(f32[3,200,128]{2,1,0:T(8,128)} %get-tuple-element.6.a, f32[1,128]{1,0:T(1,128)} %get-tuple-element.7.b), custom_call_target="tpu_custom_call" | custom-call | tf_op jit(solution)/shard_map/hand_over/pallas_call | solution.py:569

commit v2 on v1

--- a/solution.py
+++ b/solution.py
@@ -131,6 +131,16 @@
         onto = (pf[a : a + 1, 0:FACE] == down).astype(F32)
         snd[400 * a : 400 * a + FACE, :] = jnp.dot(onto, rv[a], precision=HIGHEST, preferred_element_type=F32)
 
+    pl.semaphore_wait(barrier, 32)
+
+    def face_copy(src, dst, turn, face):
+        rows = pl.ds(FACE * face, FACE)
+        return remote(src.at[rows], dst.at[rows], xs.at[turn], xr.at[turn], (xu, xd, yu, yd)[face])
+
+    for a in range(2):
+        remote(pf, pn.at[a], ps.at[0], pr.at[0], (xu, yu)[a]).start()
+    for f in (0, 2):
+        face_copy(snd, rx0, 0, f).start()
     lane = iota((8, 128), 1)
     mine = jnp.zeros((8, 128), F32)
     for z in range(2):
@@ -160,16 +170,6 @@
     to = over * 24 + up * 6 + (c >> 2) * 3 + (e - 3 * c)
     place = ((to == m) & (r < 120)).astype(F32).astype(BF16)
 
-    pl.semaphore_wait(barrier, 32)
-
-    def face_copy(src, dst, turn, face):
-        rows = pl.ds(FACE * face, FACE)
-        return remote(src.at[rows], dst.at[rows], xs.at[turn], xr.at[turn], (xu, xd, yu, yd)[face])
-
-    for a in range(2):
-        remote(pf, pn.at[a], ps.at[0], pr.at[0], (xu, yu)[a]).start()
-    for f in (0, 2):
-        face_copy(snd, rx0, 0, f).start()
     windows = ((0, 384), (128, 512), (384, 768), (512, 896))
     for blk, target in enumerate((xd, xu, yd, yu)):
         low, high = windows[blk]
@@ -194,8 +194,6 @@
         all_blocks.wait_recv()
         all_blocks.wait_send()
 
-    started(p, ring, lambda q: idt, idr, ns.at[0], nr.at[0])
-
     other = device(gx, 2 * h + 1 - core)
 
     def rows_to(slot, target, turn):
@@ -204,6 +202,7 @@
     for k in (1, 7, 2, 6):
         rows_to(p, device((gx + k) & 7, gy), 0).start()
     rows_to(p, other, 2).start()
+    started(p, ring, lambda q: idt, idr, ns.at[0], nr.at[0])
 
     def rows_in(count, turn):
         some = packed.at[0:count]
@@ -373,13 +372,14 @@
         idm[...] = sum([idr[i] for i in range(1, 16)], idr[0])
         started(h, plane, lambda q: idm, ids, ns.at[1], nr.at[1])
         ids[h] = idm[...]
+        fetch[6].wait()
+        sent_x_rows(km, ks)
+        sent_y_rows(km, ks)
+
+    def b0():
         rows_in(3, 1)
         for k in range(1, 8):
             rows_to(2 * ((gx + k) & 7) + core, other, 2).start()
-        fetch[6].wait()
-        sent_x_rows(km, ks)
-
-    def b0():
         rows_in(8, 2)
         for slot in range(16):
             for k in range(12):
@@ -410,7 +410,6 @@
     kept = {}
 
     def c0():
-        sent_y_rows(km, ks)
         kept["w0"] = direction(t0, rx1, w0, 1, rx2)
         nearby = jnp.concatenate([ids[(h + 15) & 15], ids[h], ids[(h + 1) & 15]], axis=1)
         fetch[7].wait()
@@ -519,11 +518,6 @@
         out[a] = (alpha + step * ratio) * w0[rows, :] - (step * alpha) * wm[rows, :]
 
 
-def hand_over(a, b, out, red):
-    out[...] = a[...]
-    red[...] = b[...]
-
-
 def local(rhs, stiff, schur, phi, coarse, inc, pair):
     table, order = jnp.asarray(assembly_table(), BF16), jnp.asarray(order_table(), BF16)
     v = pltpu.VMEM
@@ -551,10 +545,9 @@
     ]
     any_space = pl.BlockSpec(memory_space=pl.ANY)
     in_vmem = pl.BlockSpec(memory_space=pltpu.VMEM)
-    shapes = (jax.ShapeDtypeStruct((3, FACE, LOADS), F32), jax.ShapeDtypeStruct((1, LOADS), F32))
     result, reduction = pl.pallas_call(
         kernel,
-        out_shape=shapes,
+        out_shape=(v((3, FACE, LOADS), F32), v((1, LOADS), F32)),
         in_specs=[any_space] * 5 + [pl.BlockSpec(memory_space=pltpu.SMEM)] + [any_space] * 3,
         out_specs=(in_vmem, in_vmem),
         scratch_shapes=scratch,
@@ -566,9 +559,6 @@
         rhs[0, 0, 0], stiff[0, 0, 0], schur[0, 0, 0], phi[0, 0, 0], coarse, inc[0, 0, 0],
         pair.reshape(3, 1, FACE), table, order,
     )
-    result, reduction = pl.pallas_call(
-        hand_over, out_shape=shapes, in_specs=[in_vmem] * 2, out_specs=(in_vmem, in_vmem), name="hand_over"
-    )(result, reduction)
     return result[None, None, None], reduction[0]
 
 

time: 76.9 us -> 73.6 us (0.957)
  Pallas kernels: 76.2 us -> 71.7 us
  local copies, waits for them, and re-layouts: 0 us -> 1.23 us
    pallas_call x2 -> x1, Pallas kernels: 76.2 us -> 71.7 us  [local(): pl.pallas_call(kernel, out_shape=(v((3, FACE, LOADS), F32), v((1, LOADS),...]
    unnamed x0 -> x2, local copies, waits for them, and re-layouts: none -> 1.23 us
where the time goes in v2:
time: 73.6 us; the launch traced here: 73.5 us
  Pallas kernels  71.7 us (97%)
  local copies, waits for them, and re-layouts  1.23 us (2%)
    pallas_call x1, Pallas kernels, local(): pl.pallas_call(kernel, out_shape=(v((3, FACE, LOADS), F32), v((1, LOADS),...  71.7 us

profile of v2, /device:TPU:1, one launch (start us, length us, event | category | flops | bytes accessed | tf_op | source)
XLA Modules:
  0.0 73.5 jit_solution(3665494286403278303)
XLA Ops:
  0.6 71.7 %domain_decomposition.1 = (f32[3,200,128]{2,1,0:T(8,128)S(1)}, f32[1,128]{1,0:T(1,128)S(1)}) custom-call(f32[3,200,128]{2,1,0:T(8,128)} %bitcast.12, bf16[1200,1200]{1,0:T(8,128)(2,1)} %bitcast.10, bf16[1200,1200]{1,0:T(8,128)(2,1)} %bitcast.11, bf16[24,1200]{1,0:T(8,128)(2,1)} %bitcast.13, f32[6,1536]{1,0:T(8,128)} %coarse.1, s32[8]{0:T(128)} %bitcast.15, ...), custom_call_target="tpu_custom_call" | custom-call | tf_op jit(solution)/shard_map/domain_decomposition/pallas_call | solution.py:548
  72.3 0.7 copy.13
  73.0 0.5 copy.14

commit v3 on v2

--- a/solution.py
+++ b/solution.py
@@ -367,7 +367,6 @@
         rows_to(below, device((gx + 2) & 7, gy), 1).start()
         sent_y_rows(sm, ss)
         product(ss, 2, ts)
-        send_faces(ts, rx1, 1)
         ended(idr, ns.at[0], nr.at[0])
         idm[...] = sum([idr[i] for i in range(1, 16)], idr[0])
         started(h, plane, lambda q: idm, ids, ns.at[1], nr.at[1])
@@ -380,6 +379,7 @@
         rows_in(3, 1)
         for k in range(1, 8):
             rows_to(2 * ((gx + k) & 7) + core, other, 2).start()
+        send_faces(ts, rx1, 1)
         rows_in(8, 2)
         for slot in range(16):
             for k in range(12):

time: 73.6 us -> 72 us (0.978)
  Pallas kernels: 71.7 us -> 70 us
    pallas_call x1, Pallas kernels: 71.7 us -> 70 us  [local(): pl.pallas_call(kernel, out_shape=(v((3, FACE, LOADS), F32), v((1, LOADS),...]
where the time goes in v3:
time: 72 us; the launch traced here: 71.9 us
  Pallas kernels  70 us (97%)
  local copies, waits for them, and re-layouts  1.23 us (2%)
    pallas_call x1, Pallas kernels, local(): pl.pallas_call(kernel, out_shape=(v((3, FACE, LOADS), F32), v((1, LOADS),...  70 us

profile of v3, /device:TPU:1, one launch (start us, length us, event | category | flops | bytes accessed | tf_op | source)
XLA Modules:
  0.0 71.9 jit_solution(17229422524998287191)
XLA Ops:
  0.6 70.0 %domain_decomposition.1 = (f32[3,200,128]{2,1,0:T(8,128)S(1)}, f32[1,128]{1,0:T(1,128)S(1)}) custom-call(f32[3,200,128]{2,1,0:T(8,128)} %bitcast.12, bf16[1200,1200]{1,0:T(8,128)(2,1)} %bitcast.10, bf16[1200,1200]{1,0:T(8,128)(2,1)} %bitcast.11, bf16[24,1200]{1,0:T(8,128)(2,1)} %bitcast.13, f32[6,1536]{1,0:T(8,128)} %coarse.1, s32[8]{0:T(128)} %bitcast.15, ...), custom_call_target="tpu_custom_call" | custom-call | tf_op jit(solution)/shard_map/domain_decomposition/pallas_call | solution.py:548
  70.7 0.7 %copy.13 = f32[1,1,1,3,200,128]{5,4,3,2,1,0:T(8,128)} copy(f32[1,1,1,3,200,128]{5,4,3,2,1,0:T(8,128)S(1)} %bitcast.8) | data formatting | bytes 614400
  71.4 0.5 copy.14
